TPU v7x, 32 devices: a whole 2x2x4 slice. The times are simulated.
32 devices in a mesh: grp: 2 (over x), shard: 16 (over z, y, core).
Axes of the slice: x: 2, y: 2, z: 4, core: 2. Of those that a mesh axis runs over, the one named last changes fastest.
Arguments:
- window: bfloat16 [32, 4096], P('grp'), may hold values from -6 to 6
- weight: bfloat16 [11008, 4096], P('shard'), may hold values from -0.09375 to 0.09375
- factor_a: bfloat16 [64, 4, 4096], P(('grp', 'shard')), may hold values from -6 to 6
- factor_b: bfloat16 [64, 4, 11008], P(('grp', 'shard')), may hold values from -6 to 6
- fitness: float32 [64], P(('grp', 'shard')), may hold values from -4 to 4
Outputs:
- perturbed: bfloat16 [11008, 1024], P('shard', 'grp')
- update: float32 [11008, 4096], P('shard', 'grp')
All inputs are finite; a program needn't handle non-finite values.
Results may differ from a plain program's by a relative error of at most 0.0029.
Values may be sent and summed in bfloat16 or wider, within the bound.
A program may use at most 64 MiB of HBM per device.

v0:
```python
import math
import jax
import jax.numpy as jnp
from jax import lax
from jax.sharding import PartitionSpec as P


def contract(left_rows, right_rows):
    return lax.dot_general(
        left_rows, right_rows, (((0,), (0,)), ((), ())), preferred_element_type=jnp.float32
    )


def local(window, weight, factor_a, factor_b, fitness):
    model_width = window.shape[1]
    cand_dev, factor_rank, _ = factor_a.shape
    shard_count = lax.axis_size("shard")
    total_cands = cand_dev * lax.axis_size("grp") * shard_count
    perturb = 0.25 / math.sqrt(model_width)
    step_scale = 0.5 / math.sqrt(total_cands)
    base_out = lax.dot_general(
        weight, window, (((1,), (1,)), ((), ())), preferred_element_type=jnp.float32
    )
    projected = jnp.einsum("td,crd->crt", window, factor_a, preferred_element_type=jnp.float32)
    projected_all, fitness_all = (
        lax.all_gather(projected, "shard", axis=0, tiled=True),
        lax.all_gather(fitness, "shard", axis=0, tiled=True),
    )
    columns = lax.all_to_all(factor_b, "shard", split_axis=2, concat_axis=0, tiled=True)
    col_width = columns.shape[2]
    low_rank = jnp.einsum(
        "crt,crf->fct", projected_all, columns.astype(jnp.float32), precision=lax.Precision.HIGHEST
    )
    perturbed = (
        (base_out[:, None, :] + perturb * low_rank).astype(jnp.bfloat16).reshape(col_width, -1)
    )
    weighted = (fitness_all[:, None, None] * columns.astype(jnp.float32)).astype(jnp.bfloat16)
    exchanged = lax.all_to_all(factor_a, "grp", split_axis=2, concat_axis=0, tiled=True)
    weighted_four = weighted.reshape(shard_count, cand_dev, factor_rank, col_width)
    weighted_flat = lax.all_gather(weighted_four, "grp", axis=1, tiled=True).reshape(-1, col_width)
    owned_width = exchanged.shape[2]
    block_width = owned_width // 4
    update_parts = []
    for part_index in range(4):
        factor_slab = exchanged[:, :, part_index * block_width : (part_index + 1) * block_width]
        gathered = lax.all_gather(factor_slab, "shard", axis=0, tiled=True)
        update_parts.append(contract(weighted_flat, gathered.reshape(-1, block_width)))
    update = jnp.concatenate(update_parts, 1) * step_scale
    return (perturbed, update)


def solution(mesh):
    in_specs = (
        P("grp", None),
        P("shard", None),
        P(("grp", "shard"), None, None),
        P(("grp", "shard"), None, None),
        P(("grp", "shard")),
    )
    out_specs = (P("shard", "grp"), P("shard", "grp"))
    return jax.shard_map(local, mesh=mesh, in_specs=in_specs, out_specs=out_specs, check_vma=False)
```

profile of v0, /device:TPU:0, one launch (start us, length us, event | category | flops | bytes accessed | tf_op | source)
XLA Modules:
  0.0 226.9 jit_solution(7585882269689568177)
XLA Ops:
  0.6 4.4 %copy.14 = bf16[2,4,4096]{1,0,2:T(2,128)(2,1)S(1)} copy(bf16[2,4,4096]{2,1,0:T(4,128)(2,1)} %param.7) | data formatting | bytes 131072 | tf_op args[2]
  5.1 4.6 %reshape.41 = bf16[2,2,8192]{2,1,0:T(2,128)(2,1)} reshape(bf16[4096,2,4]{2,1,0:T(2,128)(2,1)S(1)} %bitcast.38) | data formatting | bytes 131072
  9.7 4.2 %all-to-all-start.1 = ((bf16[2,2,8192]{2,1,0:T(2,128)(2,1)}), bf16[2,2,8192]{2,1,0:T(2,128)(2,1)S(1)}, u32[]{:S(2)}, u32[]{:S(2)}) async-start(bf16[2,2,8192]{2,1,0:T(2,128)(2,1)} %reshape.41), calls=%async_computation.1 | async-start | bytes 131072 | tf_op jit(solution)/shard_map/all_to_all | solution.py:38
  13.9 4.8 %fusion.4 = f32[688,16]{0,1:T(8,128)} fusion(bf16[688,4096]{1,0:T(8,128)(2,1)} %param.6, bf16[16,4096]{1,0:T(8,128)(2,1)S(1)} %copy-done), kind=kOutput, calls=%fused_computation.7 | convolution fusion | flops 90177536 | bytes 5811200 | tf_op jit(solution)/shard_map/dot_general | solution.py:21
  19.0 9.0 %copy.12 = bf16[2,4,11008]{1,0,2:T(2,128)(2,1)} copy(bf16[2,4,11008]{2,1,0:T(4,128)(2,1)S(1)} %copy-done.3) | data formatting | bytes 352256 | tf_op args[3]
  28.0 15.1 %reshape.39 = bf16[16,2,2752]{2,1,0:T(2,128)(2,1)} reshape(bf16[11008,2,4]{2,1,0:T(2,128)(2,1)} %bitcast.36) | data formatting | bytes 352256
  44.5 34.0 %all-reduce = f32[32]{0:T(128)S(1)} all-reduce(f32[32]{0:T(128)S(1)} %dynamic-update-slice), channel_id=1, replica_groups=mesh['grp'=2,'shard'=16] {'shard'}, use_global_device_ids=true, to_apply=%add | all-reduce | flops 32 | bytes 256
  78.7 18.7 %all_gather.21 = f32[32,4,16]{2,1,0:T(4,128)} all-gather(f32[2,4,16]{2,1,0:T(4,128)S(1)} %fusion.1), channel_id=1, replica_groups=mesh['grp'=2,'shard'=16] {'shard'}, dimensions={0}, use_global_device_ids=true | all-gather | bytes 8704 | tf_op jit(solution)/shard_map/all_gather | solution.py:26
  97.4 3.5 %all-to-all-start = ((bf16[16,2,2752]{2,1,0:T(2,128)(2,1)}), bf16[16,2,2752]{2,1,0:T(2,128)(2,1)S(1)}, u32[]{:S(2)}, u32[]{:S(2)}) async-start(bf16[16,2,2752]{2,1,0:T(2,128)(2,1)} %reshape.39), calls=%async_computation | async-start | bytes 360448 | tf_op jit(solution)/shard_map/all_to_all | solution.py:29
  100.9 4.5 %reshape.42 = bf16[4096,2,4]{2,1,0:T(2,128)(2,1)S(1)} reshape(bf16[2,2,8192]{2,1,0:T(2,128)(2,1)S(1)} %all-to-all-done.1) | data formatting | bytes 131072
  105.4 1.4 copy.15
  106.9 22.4 %all_gather.24 = bf16[64,4,512]{2,1,0:T(4,128)(2,1)S(1)} all-gather(bf16[4,4,512]{2,1,0:T(4,128)(2,1)S(1)} %get-tuple-element.8), channel_id=1, replica_groups=mesh['grp'=2,'shard'=16] {'shard'}, dimensions={0}, use_global_device_ids=true | all-gather | bytes 278528 | tf_op jit(solution)/shard_map/all_gather | solution.py:46
  129.3 18.2 %all_gather.25 = bf16[64,4,512]{2,1,0:T(4,128)(2,1)S(1)} all-gather(bf16[4,4,512]{2,1,0:T(4,128)(2,1)S(1)} %get-tuple-element.11), channel_id=1, replica_groups=mesh['grp'=2,'shard'=16] {'shard'}, dimensions={0}, use_global_device_ids=true | all-gather | bytes 278528 | tf_op jit(solution)/shard_map/all_gather | solution.py:46
  148.2 19.5 %all_gather.26 = bf16[64,4,512]{2,1,0:T(4,128)(2,1)S(1)} all-gather(bf16[4,4,512]{2,1,0:T(4,128)(2,1)S(1)} %get-tuple-element.10), channel_id=1, replica_groups=mesh['grp'=2,'shard'=16] {'shard'}, dimensions={0}, use_global_device_ids=true | all-gather | bytes 278528 | tf_op jit(solution)/shard_map/all_gather | solution.py:46
  168.5 18.1 %all_gather.27 = bf16[64,4,512]{2,1,0:T(4,128)(2,1)S(1)} all-gather(bf16[4,4,512]{2,1,0:T(4,128)(2,1)S(1)} %get-tuple-element.9), channel_id=1, replica_groups=mesh['grp'=2,'shard'=16] {'shard'}, dimensions={0}, use_global_device_ids=true | all-gather | bytes 278528 | tf_op jit(solution)/shard_map/all_gather | solution.py:46
  187.4 7.4 %reshape.40 = bf16[11008,2,4]{2,1,0:T(2,128)(2,1)} reshape(bf16[16,2,2752]{2,1,0:T(2,128)(2,1)S(1)} %all-to-all-done) | data formatting | bytes 352256
  194.8 10.7 %copy.13 = bf16[2,4,16,688]{3,1,0,2:T(4,128)(2,1)S(1)} copy(bf16[2,4,16,688]{1,0,3,2:T(2,128)(2,1)} %bitcast.35) | data formatting | bytes 352256 | tf_op jit(solution)/shard_map/all_to_all | solution.py:29
  205.6 8.0 %all_gather.23 = bf16[16,4,4,688]{3,2,1,0:T(4,128)(2,1)S(1)} all-gather(bf16[16,2,4,688]{3,2,1,0:T(4,128)(2,1)S(1)} %multiply_convert_fusion), channel_id=1, replica_groups=mesh['grp'=2,'shard'=16] {'grp'}, dimensions={1}, use_global_device_ids=true | all-gather | bytes 528384 | tf_op jit(solution)/shard_map/all_gather | solution.py:40
  214.2 1.4 fusion.6
  215.6 1.5 fusion.7
  217.1 1.5 fusion.8
  218.5 1.8 fusion
  220.3 2.2 copy.16
  222.6 4.4 %maximum_multiply_fusion = f32[688,2048]{1,0:T(8,128)} fusion(f32[688,512]{1,0:T(8,128)} %fusion.8, f32[688,512]{1,0:T(8,128)} %fusion.7, f32[688,512]{1,0:T(8,128)S(1)} %fusion.6, f32[688,512]{1,0:T(8,128)S(1)} %fusion.5), kind=kLoop, calls=%fused_computation | loop fusion | flops 5636096 | bytes 11272192 | tf_op jit(solution)/shard_map/mul | solution.py:48
  (33 shorter events, 4.3 us)
Async XLA Ops:
  0.6 13.3 %copy-start = (bf16[16,4096]{1,0:T(8,128)(2,1)S(1)}, bf16[16,4096]{1,0:T(8,128)(2,1)}, u32[]{:S(2)}) copy-start(bf16[16,4096]{1,0:T(8,128)(2,1)} %param.5) | copy-start | bytes 393220
  9.7 87.7 %all-to-all-start.1 = ((bf16[2,2,8192]{2,1,0:T(2,128)(2,1)}), bf16[2,2,8192]{2,1,0:T(2,128)(2,1)S(1)}, u32[]{:S(2)}, u32[]{:S(2)}) async-start(bf16[2,2,8192]{2,1,0:T(2,128)(2,1)} %reshape.41), calls=%async_computation.1 | async-start | bytes 131072 | tf_op jit(solution)/shard_map/all_to_all | solution.py:38
  13.9 4.8 %copy-start.4 = (bf16[2,4,4096]{2,1,0:T(4,128)(2,1)S(1)}, bf16[2,4,4096]{2,1,0:T(4,128)(2,1)}, u32[]{:S(2)}) copy-start(bf16[2,4,4096]{2,1,0:T(4,128)(2,1)} %param.7) | copy-start | bytes 196612
  13.9 5.1 %copy-start.3 = (bf16[2,4,11008]{2,1,0:T(4,128)(2,1)S(1)}, bf16[2,4,11008]{2,1,0:T(4,128)(2,1)}, u32[]{:S(2)}) copy-start(bf16[2,4,11008]{2,1,0:T(4,128)(2,1)} %param.8) | copy-start | bytes 528388
  28.0 15.1 %copy-start.8 = (u32[32]{0:T(128)S(1)}, u32[32]{0:T(128)}, u32[]{:S(2)}) copy-start(u32[32]{0:T(128)} %constant.9) | copy-start | bytes 388
  28.0 16.3 %copy-start.7 = (f32[2]{0:T(128)S(1)}, f32[2]{0:T(128)}, u32[]{:S(2)}) copy-start(f32[2]{0:T(128)} %param.9) | copy-start | bytes 28
  97.4 90.0 %all-to-all-start = ((bf16[16,2,2752]{2,1,0:T(2,128)(2,1)}), bf16[16,2,2752]{2,1,0:T(2,128)(2,1)S(1)}, u32[]{:S(2)}, u32[]{:S(2)}) async-start(bf16[16,2,2752]{2,1,0:T(2,128)(2,1)} %reshape.39), calls=%async_computation | async-start | bytes 360448 | tf_op jit(solution)/shard_map/all_to_all | solution.py:29
  213.8 1.8 copy-start.1
  214.2 2.9 %copy-start.2 = (bf16[256,512]{1,0:T(8,128)(2,1)S(1)}, bf16[256,512]{1,0:T(8,128)(2,1)}, u32[]{:S(2)}) copy-start(bf16[256,512]{1,0:T(8,128)(2,1)} %reshape.32) | copy-start | bytes 786436
  215.6 3.0 %copy-start.5 = (f32[32,4,16]{2,1,0:T(4,128)S(1)}, f32[32,4,16]{2,1,0:T(4,128)}, u32[]{:S(2)}) copy-start(f32[32,4,16]{2,1,0:T(4,128)} %all_gather.21) | copy-start | bytes 24580
  215.6 3.0 %copy-start.6 = (f32[688,16]{0,1:T(8,128)S(1)}, f32[688,16]{0,1:T(8,128)}, u32[]{:S(2)}) copy-start(f32[688,16]{0,1:T(8,128)} %fusion.4) | copy-start | bytes 132100
where the time goes:
time: 228 us; the launch traced here: 227 us
  blocking collectives  139 us (61%)
  local copies, waits for them, and re-layouts  62.9 us (28%)
  matrix products  11.5 us (5%)
  starting transfers between devices  7.75 us (3%)
  other arithmetic  4.51 us (2%)
    all_gather x4, blocking collectives, local(): gathered = lax.all_gather(factor_slab, 'shard', axis=0, tiled=True)  78.1 us
    unnamed x28, local copies, waits for them, and re-layouts  48.1 us
    unnamed x1, blocking collectives  34 us
    all_gather x1, blocking collectives, local(): lax.all_gather(projected, 'shard', axis=0, tiled=True)  18.7 us
    all_to_all x1, local copies, waits for them, and re-layouts, local(): lax.all_to_all(factor_b, 'shard', split_axis=2, concat_axis=0, tiled=True)  10.7 us
    all_gather x1, blocking collectives, local(): lax.all_gather(weighted_four, 'grp', axis=1, tiled=True)  8 us
    dot_general x1, matrix products, local(): lax.dot_general(weight, window, (((1,), (1,)), ((), ())), preferred_eleme...  4.83 us
    dot_general x4, matrix products, contract(): lax.dot_general(left_rows, right_rows, (((0,), (0,)), ((), ())), preferre...  4.67 us
  transfers between devices with their start and end apart: 2, of which 0 were waited for; matrix products, arithmetic and copies ran while one was open for 17% of the time, Pallas kernels for 0%

commit v1 on v0

--- a/solution.py
+++ b/solution.py
@@ -26,7 +26,12 @@
         lax.all_gather(projected, "shard", axis=0, tiled=True),
         lax.all_gather(fitness, "shard", axis=0, tiled=True),
     )
-    columns = lax.all_to_all(factor_b, "shard", split_axis=2, concat_axis=0, tiled=True)
+    columns = jnp.concatenate(
+        lax.all_to_all(
+            jnp.stack(jnp.split(factor_b, lax.axis_size("shard"), axis=2)), "shard", 0, 0
+        ),
+        axis=0,
+    )
     col_width = columns.shape[2]
     low_rank = jnp.einsum(
         "crt,crf->fct", projected_all, columns.astype(jnp.float32), precision=lax.Precision.HIGHEST

time: 228 us -> 195 us (0.86)
  local copies, waits for them, and re-layouts: 62.9 us -> 32 us
    unnamed x28 -> x42, local copies, waits for them, and re-layouts: 48.1 us -> 27.2 us
    all_to_all x1 -> x0, local copies, waits for them, and re-layouts: 10.7 us -> none  [local(): lax.all_to_all(factor_b, 'shard', split_axis=2, concat_axis=0, tiled=True)]
  transfers between devices with their start and end apart: 2 -> 2, of which waited for: 0 -> 0; matrix products, arithmetic and copies ran while one was open for 17% -> 13% of each run, Pallas kernels for 0% -> 0%
where the time goes in v1:
time: 195 us
  blocking collectives  139 us (71%)
  local copies, waits for them, and re-layouts  32 us (16%)
  matrix products  10.5 us (5%)
  starting transfers between devices  7.76 us (4%)
  other arithmetic  4.49 us (2%)
    all_gather x4, blocking collectives, local(): gathered = lax.all_gather(factor_slab, 'shard', axis=0, tiled=True)  78.1 us
    unnamed x1, blocking collectives  34 us
    unnamed x42, local copies, waits for them, and re-layouts  27.2 us
    all_gather x1, blocking collectives, local(): lax.all_gather(projected, 'shard', axis=0, tiled=True)  18.7 us
    all_gather x1, blocking collectives, local(): lax.all_gather(weighted_four, 'grp', axis=1, tiled=True)  7.82 us
    dot_general x1, matrix products, local(): lax.dot_general(weight, window, (((1,), (1,)), ((), ())), preferred_eleme...  4.83 us
    mul x1, other arithmetic, local(): update = jnp.concatenate(update_parts, 1) * step_scale  4.35 us
    all_to_all x1, starting transfers between devices, local(): lax.all_to_all(factor_a, 'grp', split_axis=2, concat_axis=0, tiled=True)  4.23 us
  transfers between devices with their start and end apart: 2, of which 0 were waited for; matrix products, arithmetic and copies ran while one was open for 13% of the time, Pallas kernels for 0%

profile of v1, /device:TPU:0, one launch (start us, length us, event | category | flops | bytes accessed | tf_op | source)
XLA Modules:
  0.0 194.8 jit_solution(16529497137692406822)
XLA Ops:
  0.6 4.4 %copy.10 = bf16[2,4,4096]{1,0,2:T(2,128)(2,1)S(1)} copy(bf16[2,4,4096]{2,1,0:T(4,128)(2,1)} %param.7) | data formatting | bytes 131072 | tf_op args[2]
  5.1 4.6 %reshape.43 = bf16[2,2,8192]{2,1,0:T(2,128)(2,1)} reshape(bf16[4096,2,4]{2,1,0:T(2,128)(2,1)S(1)} %bitcast.60) | data formatting | bytes 131072
  9.7 4.2 %all-to-all-start.1 = ((bf16[2,2,8192]{2,1,0:T(2,128)(2,1)}), bf16[2,2,8192]{2,1,0:T(2,128)(2,1)S(1)}, u32[]{:S(2)}, u32[]{:S(2)}) async-start(bf16[2,2,8192]{2,1,0:T(2,128)(2,1)} %reshape.43), calls=%async_computation.1 | async-start | bytes 131072 | tf_op jit(solution)/shard_map/all_to_all | solution.py:43
  18.6 0.7 constant_dynamic-update-slice_fusion.8
  19.9 0.7 constant_dynamic-update-slice_fusion.6
  24.2 4.8 %fusion.3 = f32[688,16]{0,1:T(8,128)} fusion(bf16[688,4096]{1,0:T(8,128)(2,1)} %param.6, bf16[16,4096]{1,0:T(8,128)(2,1)S(1)} %copy-done), kind=kOutput, calls=%fused_computation.22 | convolution fusion | flops 90177536 | bytes 5811200 | tf_op jit(solution)/shard_map/dot_general | solution.py:21
  31.2 34.0 %all-reduce = f32[32]{0:T(128)S(1)} all-reduce(f32[32]{0:T(128)S(1)} %dynamic-update-slice), channel_id=1, replica_groups=mesh['grp'=2,'shard'=16] {'shard'}, use_global_device_ids=true, to_apply=%add | all-reduce | flops 32 | bytes 256
  65.3 18.7 %all_gather.21 = f32[32,4,16]{2,1,0:T(4,128)} all-gather(f32[2,4,16]{2,1,0:T(4,128)S(1)} %fusion), channel_id=1, replica_groups=mesh['grp'=2,'shard'=16] {'shard'}, dimensions={0}, use_global_device_ids=true | all-gather | bytes 8704 | tf_op jit(solution)/shard_map/all_gather | solution.py:26
  84.0 3.5 %all-to-all-start = ((bf16[16,2,4,688]{3,2,1,0:T(4,128)(2,1)}), bf16[16,2,4,688]{3,2,1,0:T(4,128)(2,1)S(1)}, u32[]{:S(2)}, u32[]{:S(2)}) async-start(bf16[16,2,4,688]{3,2,1,0:T(4,128)(2,1)} %constant_dynamic-update-slice_fusion), calls=%async_computation | async-start | bytes 393216 | tf_op jit(solution)/shard_map/all_to_all | solution.py:30
  87.5 4.5 %reshape.44 = bf16[4096,2,4]{2,1,0:T(2,128)(2,1)S(1)} reshape(bf16[2,2,8192]{2,1,0:T(2,128)(2,1)S(1)} %all-to-all-done.1) | data formatting | bytes 131072
  92.0 1.4 copy.11
  93.5 22.4 %all_gather.24 = bf16[64,4,512]{2,1,0:T(4,128)(2,1)S(1)} all-gather(bf16[4,4,512]{2,1,0:T(4,128)(2,1)S(1)} %get-tuple-element.8), channel_id=1, replica_groups=mesh['grp'=2,'shard'=16] {'shard'}, dimensions={0}, use_global_device_ids=true | all-gather | bytes 278528 | tf_op jit(solution)/shard_map/all_gather | solution.py:51
  115.9 18.2 %all_gather.25 = bf16[64,4,512]{2,1,0:T(4,128)(2,1)S(1)} all-gather(bf16[4,4,512]{2,1,0:T(4,128)(2,1)S(1)} %get-tuple-element.11), channel_id=1, replica_groups=mesh['grp'=2,'shard'=16] {'shard'}, dimensions={0}, use_global_device_ids=true | all-gather | bytes 278528 | tf_op jit(solution)/shard_map/all_gather | solution.py:51
  134.1 0.8 reshape.34
  134.9 19.5 %all_gather.26 = bf16[64,4,512]{2,1,0:T(4,128)(2,1)S(1)} all-gather(bf16[4,4,512]{2,1,0:T(4,128)(2,1)S(1)} %get-tuple-element.10), channel_id=1, replica_groups=mesh['grp'=2,'shard'=16] {'shard'}, dimensions={0}, use_global_device_ids=true | all-gather | bytes 278528 | tf_op jit(solution)/shard_map/all_gather | solution.py:51
  154.3 0.8 reshape.35
  155.1 18.1 %all_gather.27 = bf16[64,4,512]{2,1,0:T(4,128)(2,1)S(1)} all-gather(bf16[4,4,512]{2,1,0:T(4,128)(2,1)S(1)} %get-tuple-element.9), channel_id=1, replica_groups=mesh['grp'=2,'shard'=16] {'shard'}, dimensions={0}, use_global_device_ids=true | all-gather | bytes 278528 | tf_op jit(solution)/shard_map/all_gather | solution.py:51
  173.2 0.8 reshape.36
  174.1 7.8 %all_gather.23 = bf16[16,4,4,688]{3,2,1,0:T(4,128)(2,1)S(1)} all-gather(bf16[16,2,4,688]{3,2,1,0:T(4,128)(2,1)S(1)} %multiply_convert_fusion), channel_id=1, replica_groups=mesh['grp'=2,'shard'=16] {'grp'}, dimensions={1}, use_global_device_ids=true | all-gather | bytes 528384 | tf_op jit(solution)/shard_map/all_gather | solution.py:45
  183.5 1.5 fusion.6
  185.0 1.5 fusion.7
  186.5 1.7 add_convert_fusion
  188.2 2.2 %copy.12 = bf16[688,512]{1,0:T(8,128)(2,1)} copy(bf16[688,512]{0,1:T(8,128)(2,1)} %bitcast.61) | data formatting | bytes 1409024
  190.4 4.4 %maximum_multiply_fusion = f32[688,2048]{1,0:T(8,128)} fusion(f32[688,512]{1,0:T(8,128)} %fusion.7, f32[688,512]{1,0:T(8,128)} %fusion.6, f32[688,512]{1,0:T(8,128)S(1)} %fusion.5, f32[688,512]{1,0:T(8,128)S(1)} %fusion.4), kind=kLoop, calls=%fused_computation | loop fusion | flops 5636096 | bytes 11272192 | tf_op jit(solution)/shard_map/mul | solution.py:53
  (47 shorter events, 12.2 us)
Async XLA Ops:
  0.6 23.3 %copy-start = (bf16[16,4096]{1,0:T(8,128)(2,1)S(1)}, bf16[16,4096]{1,0:T(8,128)(2,1)}, u32[]{:S(2)}) copy-start(bf16[16,4096]{1,0:T(8,128)(2,1)} %param.5) | copy-start | bytes 393220
  5.1 8.9 %copy-start.4 = (bf16[2,4,11008]{2,1,0:T(4,128)(2,1)S(1)}, bf16[2,4,11008]{2,1,0:T(4,128)(2,1)}, u32[]{:S(2)}) copy-start(bf16[2,4,11008]{2,1,0:T(4,128)(2,1)} %param.8) | copy-start | bytes 528388
  5.1 18.9 %copy-start.5 = (bf16[2,4,4096]{2,1,0:T(4,128)(2,1)S(1)}, bf16[2,4,4096]{2,1,0:T(4,128)(2,1)}, u32[]{:S(2)}) copy-start(bf16[2,4,4096]{2,1,0:T(4,128)(2,1)} %param.7) | copy-start | bytes 196612
  9.7 74.3 %all-to-all-start.1 = ((bf16[2,2,8192]{2,1,0:T(2,128)(2,1)}), bf16[2,2,8192]{2,1,0:T(2,128)(2,1)S(1)}, u32[]{:S(2)}, u32[]{:S(2)}) async-start(bf16[2,2,8192]{2,1,0:T(2,128)(2,1)} %reshape.43), calls=%async_computation.1 | async-start | bytes 131072 | tf_op jit(solution)/shard_map/all_to_all | solution.py:43
  24.2 5.5 %copy-start.9 = (u32[32]{0:T(128)S(1)}, u32[32]{0:T(128)}, u32[]{:S(2)}) copy-start(u32[32]{0:T(128)} %constant.9) | copy-start | bytes 388
  24.2 6.8 %copy-start.8 = (f32[2]{0:T(128)S(1)}, f32[2]{0:T(128)}, u32[]{:S(2)}) copy-start(f32[2]{0:T(128)} %param.9) | copy-start | bytes 28
  84.0 90.0 %all-to-all-start = ((bf16[16,2,4,688]{3,2,1,0:T(4,128)(2,1)}), bf16[16,2,4,688]{3,2,1,0:T(4,128)(2,1)S(1)}, u32[]{:S(2)}, u32[]{:S(2)}) async-start(bf16[16,2,4,688]{3,2,1,0:T(4,128)(2,1)} %constant_dynamic-update-slice_fusion), calls=%async_computation | async-start | bytes 393216 | tf_op jit(solution)/shard_map/all_to_all | solution.py:30
  182.1 1.0 copy-start.1
  182.1 1.3 copy-start.2
  183.1 1.9 copy-start.3
  183.5 3.0 %copy-start.6 = (f32[32,4,16]{2,1,0:T(4,128)S(1)}, f32[32,4,16]{2,1,0:T(4,128)}, u32[]{:S(2)}) copy-start(f32[32,4,16]{2,1,0:T(4,128)} %all_gather.21) | copy-start | bytes 24580
  183.5 3.0 %copy-start.7 = (f32[688,16]{0,1:T(8,128)S(1)}, f32[688,16]{0,1:T(8,128)}, u32[]{:S(2)}) copy-start(f32[688,16]{0,1:T(8,128)} %fusion.3) | copy-start | bytes 132100
